TPU v7x, 32 devices: a whole 2x2x4 slice. The times are simulated.
32 devices in a mesh: rows: 8 (over y, x, core), feat: 4 (over z).
Axes of the slice: x: 2, y: 2, z: 4, core: 2. Of those that a mesh axis runs over, the one named last changes fastest.
Arguments:
- features: bfloat16 [8192, 2048], P('rows', 'feat'), may hold values from -6 to 6
- grad_out: bfloat16 [8192, 2048], P('rows', 'feat'), may hold values from -6 to 6
- eigvecs: float32 [2048, 2048], P('feat', 'rows'), may hold values from -1 to 1, as said below
- eigvals: float32 [2048], replicated, may hold values from 0.1 to 1, as said below
- whiten: bfloat16 [2048, 2048], P(None, 'feat'), may hold values from -0.125 to 0.125
Outputs:
- grad_in: bfloat16 [8192, 2048], P('rows', 'feat')
Inputs may be any that keep to these rules, and one draw needn't show every extreme that they name: `eigvecs`: the columns are orthonormal. `eigvals`: any two entries differ by at least 0.45 / 2048.
All inputs are finite; a program needn't handle non-finite values.
Results may differ from a plain program's by a relative error of at most 0.0074.
Values may be sent and summed in bfloat16 or wider, within the bound.
A program may use at most 128 MiB of HBM per device.

v0:
```python
import jax
import jax.numpy as jnp
from jax import lax
from jax.sharding import PartitionSpec as P


def divided(lam_row, lam_col, first_col):
    on_diag = (
        jnp.arange(lam_row.shape[0], dtype=jnp.int32)[:, None]
        == (first_col + jnp.arange(lam_col.shape[0], dtype=jnp.int32))[None, :]
    )
    root_row = lam_row ** (-0.5)
    root_col = lam_col ** (-0.5)
    gaps_lam = lam_row[:, None] - lam_col[None, :]
    safe_gap = jnp.where(on_diag, jnp.ones_like(gaps_lam), gaps_lam)
    off_diag = (root_row[:, None] - root_col[None, :]) / safe_gap
    diag_vals = -0.5 * lam_row[:, None] ** (-1.5) + jnp.zeros_like(gaps_lam)
    return jnp.where(on_diag, diag_vals, off_diag)


def local(features, grad_out, eigvecs, eigvals, whiten):
    highest = lax.Precision.HIGHEST
    tok_rows, own_cols = features.shape
    row_count = tok_rows * lax.axis_size("rows")
    contract_rows = (((0,), (0,)), ((), ()))
    contract_last = (((1,), (1,)), ((), ()))
    piece_x = lax.all_gather(features, "feat", axis=1, tiled=True)
    piece_g = lax.all_gather(grad_out, "feat", axis=1, tiled=True)
    left_part = lax.dot_general(
        features, piece_g, contract_rows, preferred_element_type=jnp.float32
    )
    right_part = lax.dot_general(
        grad_out, piece_x, contract_rows, preferred_element_type=jnp.float32
    )
    cross_one = left_part
    cross_two = right_part
    sum_x = jnp.sum(piece_x, axis=0, dtype=jnp.float32)
    sum_g = jnp.sum(piece_g, axis=0, dtype=jnp.float32)
    cross_one, cross_two, sum_x, sum_g = (cross_one, cross_two, sum_x, sum_g)
    cross_one, cross_two, sum_x, sum_g = lax.psum((cross_one, cross_two, sum_x, sum_g), "rows")
    both_cross = cross_one + cross_two
    col_mean = sum_x / row_count
    grad_mean = sum_g / row_count
    offset = lax.axis_index("feat") * own_cols
    mean_part = lax.dynamic_slice_in_dim(col_mean, offset, own_cols)
    grad_part = lax.dynamic_slice_in_dim(grad_mean, offset, own_cols)
    sym_gram = 0.5 * (
        both_cross
        - row_count
        * (mean_part[:, None] * grad_mean[None, :] + grad_part[:, None] * col_mean[None, :])
    )
    basis_cols = lax.all_gather(eigvecs, "feat", axis=0, tiled=True)
    basis_block = lax.all_gather(eigvecs, "rows", axis=1, tiled=True)
    narrow = basis_cols.shape[1]
    inner_prod = jnp.dot(sym_gram, basis_cols, precision=highest)
    partial_value = lax.dot_general(basis_block, inner_prod, contract_rows, precision=highest)
    rotated = lax.psum(partial_value, "feat")
    first_col = lax.axis_index("rows") * narrow
    lam_col = lax.dynamic_slice_in_dim(eigvals, first_col, narrow)
    scaled = divided(eigvals, lam_col, first_col) * rotated
    back_rot = jnp.dot(basis_block, scaled, precision=highest)
    sens_own = lax.psum_scatter(
        lax.dot_general(back_rot, basis_cols, contract_last, precision=highest),
        "rows",
        scatter_dimension=0,
        tiled=True,
    )
    scaled_own = (2.0 / row_count * sens_own).astype(jnp.bfloat16)
    sens_scaled = lax.all_gather(scaled_own, "rows", axis=0, tiled=True)
    piece_x = lax.all_gather(features, "feat", axis=1, tiled=True)
    piece_g = lax.all_gather(grad_out, "feat", axis=1, tiled=True)
    shifted = (piece_g.astype(jnp.float32) - grad_mean).astype(jnp.bfloat16)
    centered = (piece_x.astype(jnp.float32) - col_mean).astype(jnp.bfloat16)
    running = jnp.dot(shifted, whiten, preferred_element_type=jnp.float32)
    grad_in = running + lax.dot_general(
        centered, sens_scaled, contract_last, preferred_element_type=jnp.float32
    )
    return grad_in.astype(jnp.bfloat16)


def solution(mesh):
    in_specs = (P("rows", "feat"), P("rows", "feat"), P("feat", "rows"), P(), P(None, "feat"))
    out_specs = P("rows", "feat")
    return jax.shard_map(local, mesh=mesh, in_specs=in_specs, out_specs=out_specs, check_vma=False)
```

profile of v0, /device:TPU:0, one launch (start us, length us, event | category | flops | bytes accessed | tf_op | source)
XLA Modules:
  0.0 552.3 jit_solution(13871746332786428748)
XLA Ops:
  6.5 0.0 copy-start
  6.5 0.0 all-gather.6.cloned.1.call-start
  6.5 0.7 all-gather.6.cloned.1.call-update
  7.3 0.0 all-gather.8.cloned.1.call-start
  7.3 0.7 all-gather.8.cloned.1.call-update
  8.0 0.0 all-gather.10.cloned.1.call-start
  8.1 0.7 all-gather.10.cloned.1.call-update
  8.7 0.0 copy-start.3
  8.8 0.0 all-reduce.6.cloned.1.call-start
  8.8 83.6 %all-gather.6.cloned.1.call-done = bf16[1024,2048]{1,0:T(8,128)(2,1)} async-done(((bf16[1024,512]{1,0:T(8,128)(2,1)}), bf16[1024,2048]{1,0:T(8,128)(2,1)}) %all-gather.6.cloned.1.call-update) | async-done | bytes 4194320 | tf_op jit(solution)/shard_map/all_gather | solution.py:71
  92.4 6.8 %fusion.40 = f32[512,2048]{1,0:T(8,128)} fusion(bf16[1024,512]{1,0:T(8,128)(2,1)} %param.5, bf16[1024,2048]{1,0:T(8,128)(2,1)} %all-gather.6.cloned.1.call-done), kind=kOutput, calls=%fused_computation.51 | convolution fusion | flops 2147483648 | bytes 9437184 | tf_op jit(solution)/shard_map/dot_general | solution.py:29
  99.2 74.0 %all-gather.8.cloned.1.call-done = bf16[1024,2048]{1,0:T(8,128)(2,1)} async-done(((bf16[1024,512]{1,0:T(8,128)(2,1)}), bf16[1024,2048]{1,0:T(8,128)(2,1)}) %all-gather.8.cloned.1.call-update) | async-done | bytes 4194320 | tf_op jit(solution)/shard_map/all_gather | solution.py:70
  173.2 0.0 copy-done.3
  173.2 7.8 %convolution_add_fusion = f32[512,2048]{1,0:T(8,128)} fusion(f32[512,2048]{1,0:T(8,128)} %fusion.40, bf16[1024,512]{1,0:T(8,128)(2,1)S(1)} %copy-done.3, bf16[1024,2048]{1,0:T(8,128)(2,1)} %all-gather.8.cloned.1.call-done), kind=kOutput, calls=%fused_computation.17 | convolution fusion | flops 2148532224 | bytes 13631488 | tf_op jit(solution)/shard_map/dot_general | solution.py:32
  181.0 0.0 all-reduce.6.cloned.1.call-update
  181.1 0.0 all-gather.12.cloned.1.call-start
  181.1 0.5 all-gather.12.cloned.1.call-update
  181.7 0.0 all-reduce.4.cloned.1.call-start
  181.7 0.0 copy-start.1
  181.7 3.0 convert_reduce_fusion
  184.7 0.5 copy-done.1
  185.2 0.6 convert_reduce_fusion.1
  185.8 25.6 %all-reduce = (f32[2048]{0:T(1024)S(1)}, f32[2048]{0:T(1024)S(1)}) all-reduce(f32[2048]{0:T(1024)S(1)} %convert_reduce_fusion, f32[2048]{0:T(1024)S(1)} %convert_reduce_fusion.1), channel_id=1, replica_groups=mesh['rows'=8,'feat'=4] {'rows'}, use_global_device_ids=true, to_apply=%region_3.0 | all-reduce | flops 4096 | bytes 32768 | tf_op jit(solution)/shard_map/psum | solution.py:40
  211.4 0.1 dynamic_slice.10
  211.5 0.1 dynamic_slice.11
  211.6 7.4 %all-gather.10.cloned.1.call-done = f32[2048,256]{1,0:T(8,128)} async-done(((f32[512,256]{1,0:T(8,128)}), f32[2048,256]{1,0:T(8,128)}) %all-gather.10.cloned.1.call-update) | async-done | bytes 2097168 | tf_op jit(solution)/shard_map/all_gather | solution.py:52
  219.0 82.8 %all-reduce.6.cloned.1.call-done = f32[512,2048]{1,0:T(8,128)} async-done(((f32[512,2048]{1,0:T(8,128)}), f32[512,2048]{1,0:T(8,128)}) %all-reduce.6.cloned.1.call-update) | async-done | bytes 4194320 | tf_op jit(solution)/shard_map/psum | solution.py:40
  301.7 6.9 %fusion.6 = f32[512,256]{1,0:T(8,128)S(1)} fusion(f32[2048,256]{1,0:T(8,128)} %all-gather.10.cloned.1.call-done, f32[512,2048]{1,0:T(8,128)} %all-reduce.6.cloned.1.call-done, f32[2048]{0:T(1024)S(1)} %get-tuple-element.11, f32[512]{0:T(512)S(1)} %dynamic_slice.11, f32[2048]{0:T(1024)S(1)} %get-tuple-element.12, f32[512]{0:T(512)S(1)} %dynamic_slice.10), kind=kOutput, calls=%fused_computation.8 | convolution fusion | flops 3227516928 | bytes 6836224 | tf_op jit(solution)/shard_map/dot_general | solution.py:55
  308.6 0.0 copy-start.5
  308.6 32.3 %all-gather.12.cloned.1.call-done = f32[512,2048]{1,0:T(8,128)} async-done(((f32[512,256]{1,0:T(8,128)}), f32[512,2048]{1,0:T(8,128)}) %all-gather.12.cloned.1.call-update) | async-done | bytes 4194320 | tf_op jit(solution)/shard_map/all_gather | solution.py:53
  340.9 10.2 %convolution_bitcast_fusion = f32[2048,256]{1,0:T(8,128)} fusion(f32[512,256]{1,0:T(8,128)S(1)} %fusion.6, f32[512,2048]{1,0:T(8,128)} %all-gather.12.cloned.1.call-done), kind=kOutput, calls=%fused_computation.18 | convolution fusion | flops 3221225472 | bytes 6815744 | tf_op jit(solution)/shard_map/dot_general | solution.py:56
  351.1 0.0 all-reduce.4.cloned.1.call-update
  351.1 0.3 reduce-scatter.2.cloned.1.call-start
  351.4 0.0 copy-done.5
  351.4 0.1 broadcast_power_fusion.1
  351.5 85.9 %all-reduce.4.cloned.1.call-done = f32[2048,256]{1,0:T(8,128)} async-done(((f32[2048,256]{1,0:T(8,128)}), f32[2048,256]{1,0:T(8,128)}) %all-reduce.4.cloned.1.call-update) | async-done | bytes 2097168 | tf_op jit(solution)/shard_map/psum | solution.py:57
  437.4 0.0 copy-start.4
  437.4 10.8 %fusion.15 = f32[256,512]{1,0:T(8,128)S(1)} fusion(f32[512,2048]{1,0:T(8,128)} %all-gather.12.cloned.1.call-done, f32[2048,256]{1,0:T(8,128)} %all-reduce.4.cloned.1.call-done, f32[256]{0:T(256)S(1)} %get-tuple-element.8, f32[2048]{0:T(1024)S(1)} %copy-done.5, f32[256]{0:T(256)S(1)} %get-tuple-element.7, f32[2048]{0:T(1024)S(1)} %get-tuple-element.10, ...), kind=kOutput, calls=%fused_computation.20 | convolution fusion | flops 3224895488 | bytes 6843392 | tf_op jit(solution)/shard_map/dot_general | solution.py:61
  448.2 0.0 copy-done.4
  448.2 8.4 %fusion.41 = f32[512,2048]{1,0:T(8,128)} fusion(f32[256,512]{1,0:T(8,128)S(1)} %fusion.15, f32[2048,256]{1,0:T(8,128)S(1)} %copy-done.4), kind=kOutput, calls=%fused_computation.52 | convolution fusion | flops 3221225472 | bytes 6815744 | tf_op jit(solution)/shard_map/dot_general | solution.py:63
  456.6 0.0 reduce-scatter.2.cloned.1.call-update
  456.7 0.3 all-gather.14.cloned.1.call-start
  457.0 50.0 %reduce-scatter.2.cloned.1.call-done = f32[64,2048]{1,0:T(8,128)} async-done(((f32[512,2048]{1,0:T(8,128)}), f32[64,2048]{1,0:T(8,128)}) %reduce-scatter.2.cloned.1.call-update) | async-done | bytes 524304 | tf_op jit(solution)/shard_map/reduce_scatter | solution.py:62
  507.0 1.8 multiply_convert_fusion
  508.8 0.0 all-gather.14.cloned.1.call-update
  508.8 27.9 %all-gather.14.cloned.1.call-done = bf16[512,2048]{1,0:T(8,128)(2,1)} async-done(((bf16[64,2048]{1,0:T(8,128)(2,1)}), bf16[512,2048]{1,0:T(8,128)(2,1)}) %all-gather.14.cloned.1.call-update) | async-done | bytes 2097168 | tf_op jit(solution)/shard_map/all_gather | solution.py:69
  536.7 0.0 copy-start.2
  536.7 5.4 fusion.2
  542.1 0.0 copy-done
  542.1 0.0 copy-done.2
  542.1 3.3 add_convert_fusion
  (3 shorter events, 0.0 us)
Async XLA Ops:
  6.5 535.6 %copy-start = (bf16[2048,512]{1,0:T(8,128)(2,1)S(1)}, bf16[2048,512]{1,0:T(8,128)(2,1)}, u32[]{:S(2)}) copy-start(bf16[2048,512]{1,0:T(8,128)(2,1)} %param.9) | copy-start | bytes 6291460
  6.5 85.9 %all-gather.6.cloned.1.call-start = ((), (), s32[]{:S(2)}) async-start(), calls=%async_computation.1 | async-start | bytes 5242880 | tf_op jit(solution)/shard_map/all_gather | solution.py:71
  7.3 166.0 %all-gather.8.cloned.1.call-start = ((), (), s32[]{:S(2)}) async-start(), calls=%async_computation.2 | async-start | bytes 5242880 | tf_op jit(solution)/shard_map/all_gather | solution.py:70
  8.0 211.0 %all-gather.10.cloned.1.call-start = ((), (), s32[]{:S(2)}) async-start(), calls=%async_computation.3 | async-start | bytes 2621440 | tf_op jit(solution)/shard_map/all_gather | solution.py:52
  8.7 164.5 %copy-start.3 = (bf16[1024,512]{1,0:T(8,128)(2,1)S(1)}, bf16[1024,512]{1,0:T(8,128)(2,1)}, u32[]{:S(2)}) copy-start(bf16[1024,512]{1,0:T(8,128)(2,1)} %param.6) | copy-start | bytes 3145732
  8.8 293.0 %all-reduce.6.cloned.1.call-start = ((), (), s32[]{:S(2)}) async-start(), calls=%async_computation.8 | async-start | bytes 8388608 | tf_op jit(solution)/shard_map/psum | solution.py:40
  181.1 159.9 %all-gather.12.cloned.1.call-start = ((), (), s32[]{:S(2)}) async-start(), calls=%async_computation.4 | async-start | bytes 4718592 | tf_op jit(solution)/shard_map/all_gather | solution.py:53
  181.7 255.8 %all-reduce.4.cloned.1.call-start = ((), (), s32[]{:S(2)}) async-start(), calls=%async_computation.5 | async-start | bytes 4194304 | tf_op jit(solution)/shard_map/psum | solution.py:57
  181.7 3.5 copy-start.1
  308.6 42.8 %copy-start.5 = (f32[2048]{0:T(1024)S(1)}, f32[2048]{0:T(1024)}, u32[]{:S(2)}) copy-start(f32[2048]{0:T(1024)} %param.8) | copy-start | bytes 24580
  351.1 155.9 %reduce-scatter.2.cloned.1.call-start = ((), (), s32[]{:S(2)}) async-start(), calls=%async_computation.6 | async-start | bytes 4718592 | tf_op jit(solution)/shard_map/reduce_scatter | solution.py:62
  437.4 10.8 %copy-start.4 = (f32[2048,256]{1,0:T(8,128)S(1)}, f32[2048,256]{1,0:T(8,128)}, u32[]{:S(2)}) copy-start(f32[2048,256]{1,0:T(8,128)} %all-gather.10.cloned.1.call-done) | copy-start | bytes 6291460
  456.7 80.1 %all-gather.14.cloned.1.call-start = ((), (), s32[]{:S(2)}) async-start(), calls=%async_computation.7 | async-start | bytes 2359296 | tf_op jit(solution)/shard_map/all_gather | solution.py:69
  536.7 5.4 copy-start.2
Sparse Core Ops, SparseCore 0:
  8.9 83.4 all-gather.5
  94.0 79.2 all-gather.7
  174.8 44.1 all-gather.9
  222.1 79.5 all-reduce.5
  303.5 37.3 all-gather.11
  351.3 86.1 all-reduce.3
  456.8 50.1 reduce-scatter.1
  508.9 27.7 all-gather.13
where the time goes:
time: 552 us
  waiting for transfers between devices  447 us (81%)
  matrix products  59.6 us (11%)
  blocking collectives  25.6 us (5%)
  between operations  13.6 us (2%)
    psum x1, waiting for transfers between devices, local(): rotated = lax.psum(partial_value, 'feat')  85.9 us
    all_gather x1, waiting for transfers between devices, local(): piece_g = lax.all_gather(grad_out, 'feat', axis=1, tiled=True)  83.6 us
    psum x1, waiting for transfers between devices, local(): lax.psum((cross_one, cross_two, sum_x, sum_g), 'rows')  82.8 us
    all_gather x1, waiting for transfers between devices, local(): piece_x = lax.all_gather(features, 'feat', axis=1, tiled=True)  74 us
    reduce_scatter x1, waiting for transfers between devices, local(): lax.psum_scatter(lax.dot_general(back_rot, basis_cols, contract_last, pre...  50 us
    all_gather x1, waiting for transfers between devices, local(): basis_block = lax.all_gather(eigvecs, 'rows', axis=1, tiled=True)  32.3 us
    all_gather x1, waiting for transfers between devices, local(): sens_scaled = lax.all_gather(scaled_own, 'rows', axis=0, tiled=True)  27.9 us
    psum x1, blocking collectives, local(): lax.psum((cross_one, cross_two, sum_x, sum_g), 'rows')  25.6 us
  transfers between devices with their start and end apart: 8, of which 8 were waited for; matrix products, arithmetic and copies ran while one was open for 5% of the time, Pallas kernels for 0%

commit v1 on v0

--- a/solution.py
+++ b/solution.py
@@ -2,6 +2,12 @@
 import jax.numpy as jnp
 from jax import lax
 from jax.sharding import PartitionSpec as P
+
+
+def gather_and_add(value, axis):
+    blocks = lax.all_gather(value, axis, axis=0, tiled=False)
+    total = blocks.sum(axis=0)
+    return total
 
 
 def divided(lam_row, lam_col, first_col):
@@ -54,7 +60,7 @@
     narrow = basis_cols.shape[1]
     inner_prod = jnp.dot(sym_gram, basis_cols, precision=highest)
     partial_value = lax.dot_general(basis_block, inner_prod, contract_rows, precision=highest)
-    rotated = lax.psum(partial_value, "feat")
+    rotated = gather_and_add(partial_value, "feat")
     first_col = lax.axis_index("rows") * narrow
     lam_col = lax.dynamic_slice_in_dim(eigvals, first_col, narrow)
     scaled = divided(eigvals, lam_col, first_col) * rotated

time: 552 us -> 630 us (1.14)
  waiting for transfers between devices: 447 us -> 510 us
  local copies, waits for them, and re-layouts: 0.75 us -> 11.6 us
  other arithmetic: 5.43 us -> 15.4 us
    all_gather x0 -> x1, waiting for transfers between devices: none -> 150 us  [gather_and_add(): blocks = lax.all_gather(value, axis, axis=0, tiled=False)]
    psum x1 -> x0, waiting for transfers between devices: 85.9 us -> none  [local(): rotated = lax.psum(partial_value, 'feat')]
    all_gather x0 -> x1, local copies, waits for them, and re-layouts: none -> 10.8 us  [gather_and_add(): blocks = lax.all_gather(value, axis, axis=0, tiled=False)]
    reduce_sum x0 -> x1, other arithmetic: none -> 9.98 us  [gather_and_add(): total = blocks.sum(axis=0)]
  transfers between devices with their start and end apart: 8 -> 8, of which waited for: 8 -> 8; matrix products, arithmetic and copies ran while one was open for 5% -> 4% of each run, Pallas kernels for 0% -> 0%
where the time goes in v1:
time: 630 us
  waiting for transfers between devices  510 us (81%)
  matrix products  53.6 us (9%)
  blocking collectives  25.6 us (4%)
  other arithmetic  15.4 us (2%)
  between operations  13.6 us (2%)
  local copies, waits for them, and re-layouts  11.6 us (2%)
    all_gather x1, waiting for transfers between devices, gather_and_add(): blocks = lax.all_gather(value, axis, axis=0, tiled=False)  150 us
    all_gather x1, waiting for transfers between devices, local(): piece_g = lax.all_gather(grad_out, 'feat', axis=1, tiled=True)  83.6 us
    psum x1, waiting for transfers between devices, local(): lax.psum((cross_one, cross_two, sum_x, sum_g), 'rows')  82.8 us
    all_gather x1, waiting for transfers between devices, local(): piece_x = lax.all_gather(features, 'feat', axis=1, tiled=True)  74 us
    reduce_scatter x1, waiting for transfers between devices, local(): lax.psum_scatter(lax.dot_general(back_rot, basis_cols, contract_last, pre...  49.5 us
    all_gather x1, waiting for transfers between devices, local(): basis_block = lax.all_gather(eigvecs, 'rows', axis=1, tiled=True)  32.3 us
    all_gather x1, waiting for transfers between devices, local(): sens_scaled = lax.all_gather(scaled_own, 'rows', axis=0, tiled=True)  27.9 us
    psum x1, blocking collectives, local(): lax.psum((cross_one, cross_two, sum_x, sum_g), 'rows')  25.6 us
  transfers between devices with their start and end apart: 8, of which 8 were waited for; matrix products, arithmetic and copies ran while one was open for 4% of the time, Pallas kernels for 0%

profile of v1, /device:TPU:0, one launch (start us, length us, event | category | flops | bytes accessed | tf_op | source)
XLA Modules:
  0.0 629.7 jit_solution(17155769543071064466)
XLA Ops:
  6.5 0.0 copy-start
  6.5 0.0 all-gather.8.cloned.1.call-start
  6.5 0.7 all-gather.8.cloned.1.call-update
  7.3 0.0 all-gather.10.cloned.1.call-start
  7.3 0.7 all-gather.10.cloned.1.call-update
  8.0 0.0 all-gather.12.cloned.1.call-start
  8.1 0.7 all-gather.12.cloned.1.call-update
  8.7 0.0 copy-start.3
  8.8 0.0 all-reduce.3.cloned.1.call-start
  8.8 83.6 %all-gather.8.cloned.1.call-done = bf16[1024,2048]{1,0:T(8,128)(2,1)} async-done(((bf16[1024,512]{1,0:T(8,128)(2,1)}), bf16[1024,2048]{1,0:T(8,128)(2,1)}) %all-gather.8.cloned.1.call-update) | async-done | bytes 4194320 | tf_op jit(solution)/shard_map/all_gather | solution.py:77
  92.4 6.9 %fusion.40 = f32[512,2048]{1,0:T(8,128)} fusion(bf16[1024,512]{1,0:T(8,128)(2,1)} %param.5, bf16[1024,2048]{1,0:T(8,128)(2,1)} %all-gather.8.cloned.1.call-done), kind=kOutput, calls=%fused_computation.51 | convolution fusion | flops 2147483648 | bytes 9437184 | tf_op jit(solution)/shard_map/dot_general | solution.py:35
  99.3 74.0 %all-gather.10.cloned.1.call-done = bf16[1024,2048]{1,0:T(8,128)(2,1)} async-done(((bf16[1024,512]{1,0:T(8,128)(2,1)}), bf16[1024,2048]{1,0:T(8,128)(2,1)}) %all-gather.10.cloned.1.call-update) | async-done | bytes 4194320 | tf_op jit(solution)/shard_map/all_gather | solution.py:76
  173.2 0.0 copy-done.3
  173.2 7.8 %convolution_add_fusion = f32[512,2048]{1,0:T(8,128)} fusion(f32[512,2048]{1,0:T(8,128)} %fusion.40, bf16[1024,512]{1,0:T(8,128)(2,1)S(1)} %copy-done.3, bf16[1024,2048]{1,0:T(8,128)(2,1)} %all-gather.10.cloned.1.call-done), kind=kOutput, calls=%fused_computation.17 | convolution fusion | flops 2148532224 | bytes 13631488 | tf_op jit(solution)/shard_map/dot_general | solution.py:38
  181.1 0.0 all-reduce.3.cloned.1.call-update
  181.1 0.0 all-gather.14.cloned.1.call-start
  181.1 0.5 all-gather.14.cloned.1.call-update
  181.7 0.0 all-gather.18.cloned.1.call-start
  181.7 0.0 copy-start.1
  181.7 3.0 convert_reduce_fusion
  184.7 0.5 copy-done.1
  185.2 0.6 convert_reduce_fusion.1
  185.9 25.6 %all-reduce = (f32[2048]{0:T(1024)S(1)}, f32[2048]{0:T(1024)S(1)}) all-reduce(f32[2048]{0:T(1024)S(1)} %convert_reduce_fusion, f32[2048]{0:T(1024)S(1)} %convert_reduce_fusion.1), channel_id=1, replica_groups=mesh['rows'=8,'feat'=4] {'rows'}, use_global_device_ids=true, to_apply=%region_3.0 | all-reduce | flops 4096 | bytes 32768 | tf_op jit(solution)/shard_map/psum | solution.py:46
  211.4 0.1 dynamic_slice.10
  211.5 0.1 dynamic_slice.11
  211.6 7.4 %all-gather.12.cloned.1.call-done = f32[2048,256]{1,0:T(8,128)} async-done(((f32[512,256]{1,0:T(8,128)}), f32[2048,256]{1,0:T(8,128)}) %all-gather.12.cloned.1.call-update) | async-done | bytes 2097168 | tf_op jit(solution)/shard_map/all_gather | solution.py:58
  219.0 82.8 %all-reduce.3.cloned.1.call-done = f32[512,2048]{1,0:T(8,128)} async-done(((f32[512,2048]{1,0:T(8,128)}), f32[512,2048]{1,0:T(8,128)}) %all-reduce.3.cloned.1.call-update) | async-done | bytes 4194320 | tf_op jit(solution)/shard_map/psum | solution.py:46
  301.7 6.9 %fusion.6 = f32[512,256]{1,0:T(8,128)S(1)} fusion(f32[2048,256]{1,0:T(8,128)} %all-gather.12.cloned.1.call-done, f32[512,2048]{1,0:T(8,128)} %all-reduce.3.cloned.1.call-done, f32[2048]{0:T(1024)S(1)} %get-tuple-element.11, f32[512]{0:T(512)S(1)} %dynamic_slice.11, f32[2048]{0:T(1024)S(1)} %get-tuple-element.12, f32[512]{0:T(512)S(1)} %dynamic_slice.10), kind=kOutput, calls=%fused_computation.8 | convolution fusion | flops 3227516928 | bytes 6836224 | tf_op jit(solution)/shard_map/dot_general | solution.py:61
  308.6 0.0 copy-start.5
  308.6 32.3 %all-gather.14.cloned.1.call-done = f32[512,2048]{1,0:T(8,128)} async-done(((f32[512,256]{1,0:T(8,128)}), f32[512,2048]{1,0:T(8,128)}) %all-gather.14.cloned.1.call-update) | async-done | bytes 4194320 | tf_op jit(solution)/shard_map/all_gather | solution.py:59
  340.9 7.2 %convolution_bitcast_fusion = f32[2048,256]{0,1:T(8,128)} fusion(f32[512,256]{1,0:T(8,128)S(1)} %fusion.6, f32[512,2048]{1,0:T(8,128)} %all-gather.14.cloned.1.call-done), kind=kOutput, calls=%fused_computation.18 | convolution fusion | flops 3221225472 | bytes 6815744 | tf_op jit(solution)/shard_map/dot_general | solution.py:62
  348.1 0.0 all-gather.18.cloned.1.call-update
  348.1 0.0 reduce-scatter.2.cloned.1.call-start
  348.2 0.0 copy-done.5
  348.2 0.1 broadcast_power_fusion.1
  348.3 149.6 %all-gather.18.cloned.1.call-done = f32[8192,256]{0,1:T(8,128)} async-done(((f32[2048,256]{0,1:T(8,128)}), f32[8192,256]{0,1:T(8,128)}) %all-gather.18.cloned.1.call-update) | async-done | bytes 8388624 | tf_op jit(solution)/shard_map/all_gather | solution.py:8
  497.9 10.8 %reshape.15 = f32[4,2048,256]{1,0,2:T(4,128)} reshape(f32[8192,256]{0,1:T(8,128)} %all-gather.18.cloned.1.call-done) | data formatting | bytes 16777216 | tf_op jit(solution)/shard_map/all_gather | solution.py:8
  508.7 10.0 %reduce_sum.29 = f32[2048,256]{0,1:T(8,128)} reduce(f32[4,2048,256]{1,0,2:T(4,128)} %reshape.15, f32[]{:T(128)} %constant.15.clone.1), dimensions={0}, to_apply=%region_6.0 | reduce | flops 1572864 | bytes 10485764 | tf_op jit(solution)/shard_map/reduce_sum | solution.py:9
  518.7 0.0 copy-start.4
  518.7 7.6 %fusion.15 = f32[256,512]{1,0:T(8,128)S(1)} fusion(f32[512,2048]{1,0:T(8,128)} %all-gather.14.cloned.1.call-done, f32[2048,256]{0,1:T(8,128)} %reduce_sum.29, f32[256]{0:T(256)S(1)} %get-tuple-element.8, f32[2048]{0:T(1024)S(1)} %copy-done.5, f32[256]{0:T(256)S(1)} %get-tuple-element.7, f32[2048]{0:T(1024)S(1)} %get-tuple-element.10, ...), kind=kOutput, calls=%fused_computation.20 | convolution fusion | flops 3224895488 | bytes 6843392 | tf_op jit(solution)/shard_map/dot_general | solution.py:67
  526.3 0.0 copy-done.4
  526.3 8.6 %fusion.41 = f32[512,2048]{1,0:T(8,128)} fusion(f32[256,512]{1,0:T(8,128)S(1)} %fusion.15, f32[2048,256]{1,0:T(8,128)S(1)} %copy-done.4), kind=kOutput, calls=%fused_computation.52 | convolution fusion | flops 3221225472 | bytes 6815744 | tf_op jit(solution)/shard_map/dot_general | solution.py:69
  534.9 0.0 reduce-scatter.2.cloned.1.call-update
  534.9 0.0 all-gather.16.cloned.1.call-start
  534.9 49.5 %reduce-scatter.2.cloned.1.call-done = f32[64,2048]{1,0:T(8,128)} async-done(((f32[512,2048]{1,0:T(8,128)}), f32[64,2048]{1,0:T(8,128)}) %reduce-scatter.2.cloned.1.call-update) | async-done | bytes 524304 | tf_op jit(solution)/shard_map/reduce_scatter | solution.py:68
  584.4 1.8 multiply_convert_fusion
  586.2 0.0 all-gather.16.cloned.1.call-update
  586.2 27.9 %all-gather.16.cloned.1.call-done = bf16[512,2048]{1,0:T(8,128)(2,1)} async-done(((bf16[64,2048]{1,0:T(8,128)(2,1)}), bf16[512,2048]{1,0:T(8,128)(2,1)}) %all-gather.16.cloned.1.call-update) | async-done | bytes 2097168 | tf_op jit(solution)/shard_map/all_gather | solution.py:75
  614.1 0.0 copy-start.2
  614.1 5.4 fusion.2
  619.5 0.0 copy-done
  619.5 0.0 copy-done.2
  619.5 3.3 add_convert_fusion
  (3 shorter events, 0.0 us)
Async XLA Ops:
  6.5 613.0 %copy-start = (bf16[2048,512]{1,0:T(8,128)(2,1)S(1)}, bf16[2048,512]{1,0:T(8,128)(2,1)}, u32[]{:S(2)}) copy-start(bf16[2048,512]{1,0:T(8,128)(2,1)} %param.9) | copy-start | bytes 6291460
  6.5 85.9 %all-gather.8.cloned.1.call-start = ((), (), s32[]{:S(2)}) async-start(), calls=%async_computation.1 | async-start | bytes 5242880 | tf_op jit(solution)/shard_map/all_gather | solution.py:77
  7.3 166.0 %all-gather.10.cloned.1.call-start = ((), (), s32[]{:S(2)}) async-start(), calls=%async_computation.2 | async-start | bytes 5242880 | tf_op jit(solution)/shard_map/all_gather | solution.py:76
  8.0 211.0 %all-gather.12.cloned.1.call-start = ((), (), s32[]{:S(2)}) async-start(), calls=%async_computation.3 | async-start | bytes 2621440 | tf_op jit(solution)/shard_map/all_gather | solution.py:58
  8.7 164.5 %copy-start.3 = (bf16[1024,512]{1,0:T(8,128)(2,1)S(1)}, bf16[1024,512]{1,0:T(8,128)(2,1)}, u32[]{:S(2)}) copy-start(bf16[1024,512]{1,0:T(8,128)(2,1)} %param.6) | copy-start | bytes 3145732
  8.8 293.0 %all-reduce.3.cloned.1.call-start = ((), (), s32[]{:S(2)}) async-start(), calls=%async_computation.8 | async-start | bytes 8388608 | tf_op jit(solution)/shard_map/psum | solution.py:46
  181.1 159.8 %all-gather.14.cloned.1.call-start = ((), (), s32[]{:S(2)}) async-start(), calls=%async_computation.4 | async-start | bytes 4718592 | tf_op jit(solution)/shard_map/all_gather | solution.py:59
  181.7 316.2 %all-gather.18.cloned.1.call-start = ((), (), s32[]{:S(2)}) async-start(), calls=%async_computation.7 | async-start | bytes 10485760 | tf_op jit(solution)/shard_map/all_gather | solution.py:8
  181.7 3.5 copy-start.1
  308.6 39.6 %copy-start.5 = (f32[2048]{0:T(1024)S(1)}, f32[2048]{0:T(1024)}, u32[]{:S(2)}) copy-start(f32[2048]{0:T(1024)} %param.8) | copy-start | bytes 24580
  348.1 236.3 %reduce-scatter.2.cloned.1.call-start = ((), (), s32[]{:S(2)}) async-start(), calls=%async_computation.5 | async-start | bytes 4718592 | tf_op jit(solution)/shard_map/reduce_scatter | solution.py:68
  518.7 7.6 %copy-start.4 = (f32[2048,256]{1,0:T(8,128)S(1)}, f32[2048,256]{1,0:T(8,128)}, u32[]{:S(2)}) copy-start(f32[2048,256]{1,0:T(8,128)} %all-gather.12.cloned.1.call-done) | copy-start | bytes 6291460
  534.9 79.2 %all-gather.16.cloned.1.call-start = ((), (), s32[]{:S(2)}) async-start(), calls=%async_computation.6 | async-start | bytes 2359296 | tf_op jit(solution)/shard_map/all_gather | solution.py:75
  614.1 5.4 copy-start.2
Sparse Core Ops, SparseCore 0:
  8.9 83.4 all-gather.7
  94.0 79.2 all-gather.9
  174.8 44.1 all-gather.11
  222.1 79.5 all-reduce.2
  303.5 37.3 all-gather.13
  348.3 149.5 all-gather.17
  535.0 49.3 reduce-scatter.1
  586.3 27.7 all-gather.15
